TPU v7x, 32 devices: a whole 2x2x4 slice. The times are simulated.
32 devices in a mesh: rad: 4 (over x, core), harm: 8 (over z, y).
Axes of the slice: x: 2, y: 2, z: 4, core: 2. Of those that a mesh axis runs over, the one named last changes fastest.
Arguments:
- velocity: bfloat16 [3, 16, 2, 256, 256], P(None, 'rad', None, 'harm'), may hold values from -6 to 6
- magnetic: bfloat16 [3, 16, 2, 256, 256], P(None, 'rad', None, 'harm'), may hold values from -6 to 6
- vorticity: bfloat16 [3, 16, 2, 256, 256], P(None, 'rad', None, 'harm'), may hold values from -6 to 6
- current: bfloat16 [3, 16, 2, 256, 256], P(None, 'rad', None, 'harm'), may hold values from -6 to 6
Outputs:
- advection: bfloat16 [3, 16, 2, 256, 256], P(None, 'rad', None, 'harm')
- induction_gradient: bfloat16 [3, 16, 2, 256, 256], P(None, 'rad', None, 'harm')
- energy_spectra: float32 [2, 16, 256], P(None, 'rad')
All inputs are finite; a program needn't handle non-finite values.
Results may differ from a plain program's by a relative error of at most 0.01.
Values may be sent and summed in bfloat16 or wider, within the bound.
A program may use at most 64 MiB of HBM per device.

v0:
```python
import functools

import jax
import jax.numpy as jnp
import numpy as np
from jax import lax
from jax.experimental import pallas as pl
from jax.experimental.pallas import tpu as pltpu
from jax.sharding import PartitionSpec as P

MESH = pl.DeviceIdType.MESH
PASSES = 2
BF = jnp.bfloat16
F32 = jnp.float32


def tables(degrees, thetas, points, harm_count):
    half = thetas // 2
    angles = np.pi * (np.arange(half) + 0.5) / thetas
    cosine = np.concatenate([np.cos(angles), -np.cos(angles)[::-1]])
    sine = np.concatenate([np.sin(angles), np.sin(angles)[::-1]])
    orders = np.arange(degrees)
    steps = np.arange(1, degrees)
    terms = 0.5 * np.log((2.0 * steps + 1.0) / (2.0 * steps))
    start = 0.5 * np.log(0.5) + np.concatenate([[0.0], np.cumsum(terms)])
    log_sector = start[:, None] + orders[:, None] * np.log(sine)[None, :]
    sectoral = np.exp(np.maximum(log_sector, -60.0)).astype(np.float32)
    unscale = np.exp(np.minimum(log_sector + 60.0, 0.0)).astype(np.float32)
    wave = np.arange(1, half + 1)
    series = np.cos(2.0 * wave[None, :] * angles[:, None]) / (4.0 * wave[None, :] ** 2 - 1.0)
    north = 2.0 / thetas * (1.0 - 2.0 * series.sum(axis=1))
    weights = np.concatenate([north, north[::-1]])
    weights = (weights * degrees / points).astype(np.float32)
    phase = 2.0 * np.pi * ((orders[:, None] * np.arange(points)[None, :]) % points) / points
    trig = np.stack([np.cos(phase), np.sin(phase)])
    trig = trig.reshape(2, harm_count, degrees // harm_count, points)
    trig = trig.transpose(1, 0, 2, 3).reshape(2 * degrees, points).astype(jnp.bfloat16)
    doubled = np.where(orders == 0, 1.0, 2.0).reshape(harm_count, 1, -1)
    doubled = np.broadcast_to(doubled, (harm_count, 2, degrees // harm_count)).reshape(-1, 1)
    analysis = (trig.astype(np.float32) * doubled).astype(jnp.bfloat16)
    return cosine.astype(np.float32), sectoral, unscale, weights, trig.T.copy(), analysis


def wide(column, width):
    return jnp.concatenate([column] * (width // column.shape[1]), axis=1)


def kernel(
    dims,
    cm_ref, x_ref, sect_ref, unscale_ref, w_ref, trig_ref, back_ref, energy_ref,
    out_ref, energy_out,
    tab, rows, outs, send, recv, grid, prod, send2, recv2, folded, spread, energy_all,
    ssem, rsem, ssem2, rsem2, esend, erecv,
):
    harm, shells, groups, modes, degrees, thetas, points, span = dims
    me = lax.axis_index("harm")
    pair_width = 2 * span
    block = min(16, modes)
    q_pairs = 6 // PASSES
    q_rows = 12 // PASSES * shells * 2

    barrier = pltpu.get_barrier_semaphore()
    for step in range(1, harm):
        peer = lax.rem(me + step, harm)
        pl.semaphore_signal(barrier, inc=1, device_id={"harm": peer}, device_id_type=MESH)

    order = (me * modes + lax.broadcasted_iota(jnp.int32, (modes, 128), 0)).astype(F32)
    order_square = order * order
    energy_all[me] = energy_ref[...]

    def table_block(step, carry):
        latest, before, inverse = carry
        for inner in range(16):
            degree = step * 16 + inner
            lf = jnp.full((modes, 128), degree, jnp.int32).astype(F32)
            dd = jnp.maximum(lf * lf - order_square, 1.0) / (4.0 * lf * lf - 1.0)
            guess = lax.rsqrt(dd)
            guess = guess * (1.5 - 0.5 * dd * guess * guess)
            live = lf > order
            alpha = jnp.where(live, guess, 0.0)
            starts = jnp.where(lf == order, 1.0, 0.0)
            new = wide(alpha, thetas) * (x_ref[...] * latest - wide(inverse, thetas) * before)
            new = new + wide(starts, thetas) * sect_ref[...]
            rows[inner] = new * unscale_ref[...]
            before, latest = latest, new
            inverse = jnp.where(live, dd * guess, 0.0)
        tab[:, pl.ds(pl.multiple_of(step * 16, 16), 16), :] = jnp.swapaxes(rows[...], 0, 1).astype(BF)
        return latest, before, inverse

    zero = jnp.zeros((modes, thetas), F32)
    lax.fori_loop(0, degrees // 16, table_block, (zero, zero, jnp.zeros((modes, 128), F32)))

    pl.semaphore_wait(barrier, harm - 1)

    def energy_copy(step):
        peer = lax.rem(me + step, harm)
        return pltpu.make_async_remote_copy(
            src_ref=energy_all.at[me], dst_ref=energy_all.at[me],
            send_sem=esend.at[step], recv_sem=erecv.at[step],
            device_id={"harm": peer}, device_id_type=MESH,
        )

    def forward(q, step):
        peer = lax.rem(me + step, harm)
        return pltpu.make_async_remote_copy(
            src_ref=send.at[peer, pl.ds(q * q_pairs, q_pairs)],
            dst_ref=recv.at[me, pl.ds(q * q_pairs, q_pairs)],
            send_sem=ssem.at[q, step], recv_sem=rsem.at[q, step],
            device_id={"harm": peer}, device_id_type=MESH,
        )

    def backward(pair, step):
        peer = lax.rem(me + step, harm)
        return pltpu.make_async_remote_copy(
            src_ref=send2.at[peer, pair], dst_ref=recv2.at[me, pair],
            send_sem=ssem2.at[pair, step], recv_sem=rsem2.at[pair, step],
            device_id={"harm": peer}, device_id_type=MESH,
        )

    for q in range(PASSES):
        def mode_block(mb, _, q=q):
            def one(i, _):
                m = mb * block + i
                outs[i] = jnp.dot(cm_ref[q, m], tab[m], preferred_element_type=F32) * (1.0 / degrees)
                return 0

            lax.fori_loop(0, block, one, 0)
            turned = jnp.swapaxes(outs[...], 0, 1)
            for s in range(shells):
                for pair in range(q_pairs):
                    for r in range(2):
                        k = (pair * 2 * shells + s) * 2 + r
                        first, second = turned[k], turned[k + 2 * shells]
                        for g in range(groups):
                            cut = slice(g * span, (g + 1) * span)
                            piece = jnp.concatenate([first[:, cut], second[:, cut]], axis=1).astype(BF)
                            at = pl.multiple_of(r * modes + mb * block, block)
                            send[s * groups + g, q * q_pairs + pair, pl.ds(at, block), :] = piece
            return 0

        lax.fori_loop(0, modes // block, mode_block, 0)
        for step in range(1, harm):
            forward(q, step).start()
        recv[me, pl.ds(q * q_pairs, q_pairs)] = send[me, pl.ds(q * q_pairs, q_pairs)]
    for step in range(1, harm):
        energy_copy(step).start()

    chunk = points // 3
    for q in range(PASSES):
        for step in range(1, harm):
            forward(q, step).wait_recv()
        for pair in range(q * q_pairs, (q + 1) * q_pairs):
            arrived = recv[:, pair].reshape(2 * degrees, pair_width)
            for part in range(3):
                cut = pl.ds(part * chunk, chunk)
                grid[pair, cut, :] = jnp.dot(trig_ref[cut, :], arrived, preferred_element_type=F32)

    piece_rows = 32

    def product_rows(i, _):
        at = pl.ds(pl.multiple_of(i * piece_rows, piece_rows), piece_rows)
        both = [grid[pair, at, :] for pair in range(6)]
        c = []
        for pair in range(6):
            c += [both[pair][:, :span], both[pair][:, span:]]
        u, b, w, j = c[0:3], c[3:6], c[6:9], c[9:12]

        def cross(a, d):
            return [a[1] * d[2] - a[2] * d[1], a[2] * d[0] - a[0] * d[2], a[0] * d[1] - a[1] * d[0]]

        lamb, lorentz, induced = cross(u, w), cross(j, b), cross(u, b)
        six = [lamb[n] + lorentz[n] for n in range(3)] + induced
        for pair in range(3):
            prod[pair, at, :] = jnp.concatenate([six[2 * pair], six[2 * pair + 1]], axis=1).astype(BF)
        return 0

    lax.fori_loop(0, points // piece_rows, product_rows, 0)

    per = 2 * modes
    for pair in range(3):
        analysed = jnp.dot(back_ref[...], prod[pair], preferred_element_type=F32)
        analysed = (analysed * w_ref[...]).astype(BF)
        send2[:, pair] = analysed.reshape(harm, per, pair_width)
        for step in range(1, harm):
            backward(pair, step).start()
        recv2[me, pair] = send2[me, pair]

    for pair in range(3):
        for step in range(1, harm):
            backward(pair, step).wait_recv()

        def fold_block(mb, _, pair=pair):
            for s in range(shells):
                for r in range(2):
                    at = pl.ds(pl.multiple_of(r * modes + mb * block, block), block)
                    got = [recv2[s * groups + g, pair, at, :].astype(F32) for g in range(groups)]
                    for c in range(2):
                        cut = slice(c * span, (c + 1) * span)
                        spread[(c * shells + s) * 2 + r] = jnp.concatenate([v[:, cut] for v in got], axis=1)
            here = pl.ds(pl.multiple_of(mb * block, block), block)
            folded[here, pl.ds(pair * 4 * shells, 4 * shells), :] = jnp.swapaxes(spread[...], 0, 1).astype(BF)
            return 0

        lax.fori_loop(0, modes // block, fold_block, 0)

    def spectrum(m, _):
        out_ref[m] = lax.dot_general(
            folded[m], tab[m], (((1,), (1,)), ((), ())), preferred_element_type=F32
        ).astype(BF)
        return 0

    lax.fori_loop(0, modes, spectrum, 0)

    for step in range(1, harm):
        energy_copy(step).wait_recv()
    energy_out[...] = jnp.sum(energy_all[...], axis=0)
    for step in range(1, harm):
        energy_copy(step).wait_send()
        for q in range(PASSES):
            forward(q, step).wait_send()
        for pair in range(3):
            backward(pair, step).wait_send()


def with_halo(block, axis):
    count = lax.axis_size(axis)
    up = [(i, i + 1) for i in range(count - 1)]
    down = [(b, a) for a, b in up]
    low = lax.ppermute(block[:, -1:], axis, up)
    high = lax.ppermute(block[:, :1], axis, down)
    return jnp.concatenate([low, block, high], axis=1)


def energy_weights(order_ints, degree_count):
    degrees = jnp.arange(degree_count, dtype=jnp.int32)
    order_col = order_ints[:, None]
    live_part = (degrees[None, :] >= order_col).astype(F32)
    inverse_modes = 1.0 / (2.0 * degrees.astype(F32) + 1.0)
    cosine_weight = jnp.where(order_col == 0, 0.5, 1.0)
    sine_weight = jnp.where(order_col == 0, 0.0, 1.0)
    scaled = live_part * inverse_modes[None, :]
    return jnp.stack([cosine_weight * scaled, sine_weight * scaled])


def local(velocity, magnetic, vorticity, current):
    harm = lax.axis_size("harm")
    me = lax.axis_index("harm")
    _, shells, _, modes, degrees = velocity.shape
    thetas, points = 3 * degrees // 2, 3 * degrees
    groups = harm // shells
    span = thetas // groups
    cosine, sectoral, unscale, weights, synthesis, analysis = tables(degrees, thetas, points, harm)

    own = me * modes + jnp.arange(modes, dtype=jnp.int32)
    energy_weight = energy_weights(own, degrees)
    energy = jnp.stack([
        jnp.sum(field.astype(F32) ** 2 * energy_weight[None, None], axis=(0, 2, 3))
        for field in (velocity, magnetic)
    ]).reshape(2 * shells, degrees)

    fields = jnp.concatenate([velocity, magnetic, vorticity, current], axis=0)
    q_rows = 12 // PASSES * shells * 2
    cm = fields.reshape(PASSES, q_rows, modes, degrees).transpose(0, 2, 1, 3)
    x = jnp.broadcast_to(jnp.asarray(cosine)[None, :], (modes, thetas))
    sect = lax.dynamic_slice_in_dim(jnp.asarray(sectoral), me * modes, modes)
    unsc = lax.dynamic_slice_in_dim(jnp.asarray(unscale), me * modes, modes)
    own_weights = lax.dynamic_slice_in_dim(jnp.asarray(weights), lax.rem(me, groups) * span, span)
    w = jnp.concatenate([own_weights, own_weights])[None, :]

    block = min(16, modes)
    vmem = pl.BlockSpec(memory_space=pltpu.VMEM)
    dims = (harm, shells, groups, modes, degrees, thetas, points, span)
    spectra, total = pl.pallas_call(
        functools.partial(kernel, dims),
        name="dynamo",
        out_shape=(
            jax.ShapeDtypeStruct((modes, 12 * shells, degrees), BF),
            jax.ShapeDtypeStruct((2 * shells, degrees), F32),
        ),
        in_specs=[vmem] * 8,
        out_specs=(vmem, vmem),
        scratch_shapes=[
            pltpu.VMEM((modes, degrees, thetas), BF),
            pltpu.VMEM((16, modes, thetas), F32),
            pltpu.VMEM((block, q_rows, thetas), F32),
            pltpu.VMEM((harm, 6, 2 * modes, 2 * span), BF),
            pltpu.VMEM((harm, 6, 2 * modes, 2 * span), BF),
            pltpu.VMEM((6, points, 2 * span), F32),
            pltpu.VMEM((3, points, 2 * span), BF),
            pltpu.VMEM((harm, 3, 2 * modes, 2 * span), BF),
            pltpu.VMEM((harm, 3, 2 * modes, 2 * span), BF),
            pltpu.VMEM((modes, 12 * shells, thetas), BF),
            pltpu.VMEM((4 * shells, block, thetas), F32),
            pltpu.VMEM((harm, 2 * shells, degrees), F32),
            pltpu.SemaphoreType.DMA((PASSES, harm)),
            pltpu.SemaphoreType.DMA((PASSES, harm)),
            pltpu.SemaphoreType.DMA((3, harm)),
            pltpu.SemaphoreType.DMA((3, harm)),
            pltpu.SemaphoreType.DMA((harm,)),
            pltpu.SemaphoreType.DMA((harm,)),
        ],
        compiler_params=pltpu.CompilerParams(
            collective_id=0, has_side_effects=True, vmem_limit_bytes=60 * 1024 * 1024
        ),
    )(cm, x, sect, unsc, w, jnp.asarray(synthesis), jnp.asarray(analysis), energy)

    spectra = spectra.transpose(1, 0, 2).reshape(6, shells, 2, modes, degrees)
    rimmed = with_halo(spectra[3:], "rad").astype(F32)
    gradient = ((rimmed[:, 2:] - rimmed[:, :-2]) * 0.5).astype(BF)
    return spectra[:3], gradient, total.reshape(2, shells, degrees)


def solution(mesh):
    spec = P(None, "rad", None, "harm", None)
    return jax.shard_map(
        local,
        mesh=mesh,
        in_specs=(spec,) * 4,
        out_specs=(spec, spec, P(None, "rad", None)),
        check_vma=False,
    )
```

profile of v0, /device:TPU:26, one launch (start us, length us, event | category | flops | bytes accessed | tf_op | source)
XLA Modules:
  0.0 129.5 jit_solution(16579087609365664307)
XLA Ops:
  0.7 1.6 %pad_maximum_fusion = bf16[12,4,2,32,256]{4,3,2,1,0:T(8,128)(2,1)S(1)} fusion(bf16[3,4,2,32,256]{4,3,2,1,0:T(8,128)(2,1)} %param.13, bf16[3,4,2,32,256]{4,3,2,1,0:T(8,128)(2,1)} %param.12, bf16[3,4,2,32,256]{4,3,2,1,0:T(8,128)(2,1)} %param.11, bf16[3,4,2,32,256]{4,3,2,1,0:T(8,128)(2,1)} %param.10), kind=kLoop, calls=%fused_computation | loop fusion | flops 2359296 | bytes 3145728 | tf_op jit(solution)/shard_map/concatenate | solution.py:261
  2.2 0.0 copy-start.4
  2.2 0.0 copy-start
  2.3 0.0 copy-start.1
  2.3 0.0 copy-start.3
  2.3 2.0 %copy.25 = bf16[2,48,32,256]{3,1,2,0:T(8,128)(2,1)} copy(bf16[2,48,32,256]{3,2,1,0:T(8,128)(2,1)S(1)} %bitcast.10) | data formatting | bytes 3145728 | tf_op jit(solution)/shard_map/reshape | solution.py:263
  4.3 0.0 copy-done.4
  4.3 0.1 dynamic_slice.11
  4.4 0.1 pad_maximum_fusion.3
  4.5 0.6 broadcast_in_dim.27.w_ref
  5.1 0.1 select_multiply_fusion.1
  5.1 0.0 copy-done
  5.2 0.0 copy-done.1
  5.2 0.2 multiply_reduce_fusion.1
  5.4 0.6 reshape.183.energy_ref
  6.0 1.5 %constant_dynamic-slice_fusion = (f32[32,384]{1,0:T(8,128)}, f32[32,384]{1,0:T(8,128)}) fusion(f32[256,384]{1,0:T(8,128)} %constant.44.clone, s32[]{:T(128)S(6)} %select_n.24, f32[256,384]{1,0:T(8,128)} %constant.43.clone), kind=kLoop, calls=%fused_computation.18 | loop fusion | bytes 196612 | tf_op jit(solution)/shard_map/dynamic_slice | solution.py:266
  7.5 0.0 copy-done.3
  7.5 0.6 broadcast_in_dim.26.x_ref
  8.1 111.3 %dynamo.1 = (bf16[32,48,256]{2,1,0:T(8,128)(2,1)}, f32[8,256]{1,0:T(8,128)}) custom-call(bf16[2,32,48,256]{3,2,1,0:T(8,128)(2,1)} %bitcast.9, f32[32,384]{1,0:T(8,128)} %broadcast_in_dim.26.x_ref, f32[32,384]{1,0:T(8,128)} %get-tuple-element.24.sect_ref, f32[32,384]{1,0:T(8,128)} %get-tuple-element.23.unscale_ref, f32[1,384]{1,0:T(1,128)} %broadcast_in_dim.27.w_ref, ...), custom_call_target="tpu_custom_call" | custom-call | tf_op jit(solution)/shard_map/dynamo/pallas_call | solution.py:273
  119.4 0.0 copy-start.2
  119.4 1.2 fusion.2
  120.6 0.1 copy.23
  120.7 1.9 %collective-permute-start.1 = (bf16[3,1,2,32,256]{4,3,2,1,0:T(8,128)(2,1)S(1)}, bf16[3,1,2,32,256]{4,3,2,1,0:T(8,128)(2,1)S(1)}, u32[]{:S(2)}, u32[]{:S(2)}) collective-permute-start(bf16[3,1,2,32,256]{4,3,2,1,0:T(8,128)(2,1)S(1)} %get-tuple-element.18), channel_id=1, source_target_pairs={{8,0},{16,8},{24,16},{9,1},{17,9},{25,17},{10,2},{18,10},{26,18},{... | collective-permute-start | bytes 294920 | tf_op jit(solution)/shard_map/ppermute | solution.py:230
  122.6 2.4 %collective-permute-start = (bf16[3,1,2,32,256]{4,3,2,1,0:T(8,128)(2,1)S(1)}, bf16[3,1,2,32,256]{4,3,2,1,0:T(8,128)(2,1)S(1)}, u32[]{:S(2)}, u32[]{:S(2)}) collective-permute-start(bf16[3,1,2,32,256]{4,3,2,1,0:T(8,128)(2,1)S(1)} %get-tuple-element.17), channel_id=1, source_target_pairs={{0,8},{8,16},{16,24},{1,9},{9,17},{17,25},{2,10},{10,18},{18,26},{... | collective-permute-start | bytes 294920 | tf_op jit(solution)/shard_map/ppermute | solution.py:229
  125.0 0.8 copy.22
  125.9 0.0 copy-done.2
  125.9 0.6 reshape.184
  126.5 0.0 collective-permute-done.1
  126.5 2.1 %collective-permute-done = bf16[3,1,2,32,256]{4,3,2,1,0:T(8,128)(2,1)S(1)} collective-permute-done((bf16[3,1,2,32,256]{4,3,2,1,0:T(8,128)(2,1)S(1)}, bf16[3,1,2,32,256]{4,3,2,1,0:T(8,128)(2,1)S(1)}, u32[]{:S(2)}, u32[]{:S(2)}) %collective-permute-start) | collective-permute-done | bytes 98336 | tf_op jit(solution)/shard_map/ppermute | solution.py:229
  128.6 0.1 maximum_convert_fusion
  128.7 0.9 fusion.1
  (6 shorter events, 0.0 us)
Async XLA Ops:
  2.2 2.1 %copy-start.4 = (f32[384]{0:T(512)S(1)}, f32[384]{0:T(512)}, u32[]{:S(2)}) copy-start(f32[384]{0:T(512)} %constant.45.clone) | copy-start | bytes 4612
  2.2 2.9 %copy-start = (bf16[3,4,2,32,256]{4,3,2,1,0:T(8,128)(2,1)S(1)}, bf16[3,4,2,32,256]{4,3,2,1,0:T(8,128)(2,1)}, u32[]{:S(2)}) copy-start(bf16[3,4,2,32,256]{4,3,2,1,0:T(8,128)(2,1)} %param.11) | copy-start | bytes 1179652
  2.3 2.9 %copy-start.1 = (bf16[3,4,2,32,256]{4,3,2,1,0:T(8,128)(2,1)S(1)}, bf16[3,4,2,32,256]{4,3,2,1,0:T(8,128)(2,1)}, u32[]{:S(2)}) copy-start(bf16[3,4,2,32,256]{4,3,2,1,0:T(8,128)(2,1)} %param.10) | copy-start | bytes 1179652
  2.3 5.2 %copy-start.3 = (f32[384]{0:T(512)S(1)}, f32[384]{0:T(512)}, u32[]{:S(2)}) copy-start(f32[384]{0:T(512)} %constant.42.clone) | copy-start | bytes 4612
  119.4 6.5 %copy-start.2 = (f32[8,256]{1,0:T(8,128)S(1)}, f32[8,256]{1,0:T(8,128)}, u32[]{:S(2)}) copy-start(f32[8,256]{1,0:T(8,128)} %get-tuple-element.6) | copy-start | bytes 24580
  120.7 5.8 %collective-permute-start.1 = (bf16[3,1,2,32,256]{4,3,2,1,0:T(8,128)(2,1)S(1)}, bf16[3,1,2,32,256]{4,3,2,1,0:T(8,128)(2,1)S(1)}, u32[]{:S(2)}, u32[]{:S(2)}) collective-permute-start(bf16[3,1,2,32,256]{4,3,2,1,0:T(8,128)(2,1)S(1)} %get-tuple-element.18), channel_id=1, source_target_pairs={{8,0},{16,8},{24,16},{9,1},{17,9},{25,17},{10,2},{18,10},{26,18},{... | collective-permute-start | bytes 294920 | tf_op jit(solution)/shard_map/ppermute | solution.py:230
  122.6 5.9 %collective-permute-start = (bf16[3,1,2,32,256]{4,3,2,1,0:T(8,128)(2,1)S(1)}, bf16[3,1,2,32,256]{4,3,2,1,0:T(8,128)(2,1)S(1)}, u32[]{:S(2)}, u32[]{:S(2)}) collective-permute-start(bf16[3,1,2,32,256]{4,3,2,1,0:T(8,128)(2,1)S(1)} %get-tuple-element.17), channel_id=1, source_target_pairs={{0,8},{8,16},{16,24},{1,9},{9,17},{17,25},{2,10},{10,18},{18,26},{... | collective-permute-start | bytes 294920 | tf_op jit(solution)/shard_map/ppermute | solution.py:229
where the time goes:
time: 130 us
  Pallas kernels  111 us (85%)
  local copies, waits for them, and re-layouts  8.11 us (6%)
  starting transfers between devices  4.33 us (3%)
  other arithmetic  2.92 us (2%)
  waiting for transfers between devices  2.08 us (2%)
    pallas_call x1, Pallas kernels, local(): pl.pallas_call(functools.partial(kernel, dims), name='dynamo', out_shape=...  111 us
  transfers between devices with their start and end apart: 2, of which 1 were waited for; matrix products, arithmetic and copies ran while one was open for 1% of the time, Pallas kernels for 0%

commit v1 on v0

--- a/solution.py
+++ b/solution.py
@@ -66,6 +66,7 @@
 
     order = (me * modes + lax.broadcasted_iota(jnp.int32, (modes, 128), 0)).astype(F32)
     order_square = order * order
+    own = pl.ds(pl.multiple_of(me * modes, modes), modes)
     energy_all[me] = energy_ref[...]
 
     def table_block(step, carry):
@@ -80,8 +81,8 @@
             alpha = jnp.where(live, guess, 0.0)
             starts = jnp.where(lf == order, 1.0, 0.0)
             new = wide(alpha, thetas) * (x_ref[...] * latest - wide(inverse, thetas) * before)
-            new = new + wide(starts, thetas) * sect_ref[...]
-            rows[inner] = new * unscale_ref[...]
+            new = new + wide(starts, thetas) * sect_ref[own, :]
+            rows[inner] = new * unscale_ref[own, :]
             before, latest = latest, new
             inverse = jnp.where(live, dd * guess, 0.0)
         tab[:, pl.ds(pl.multiple_of(step * 16, 16), 16), :] = jnp.swapaxes(rows[...], 0, 1).astype(BF)
@@ -124,7 +125,7 @@
                 outs[i] = jnp.dot(cm_ref[q, m], tab[m], preferred_element_type=F32) * (1.0 / degrees)
                 return 0
 
-            lax.fori_loop(0, block, one, 0)
+            lax.fori_loop(0, block, one, 0, unroll=4)
             turned = jnp.swapaxes(outs[...], 0, 1)
             for s in range(shells):
                 for pair in range(q_pairs):
@@ -179,7 +180,7 @@
     per = 2 * modes
     for pair in range(3):
         analysed = jnp.dot(back_ref[...], prod[pair], preferred_element_type=F32)
-        analysed = (analysed * w_ref[...]).astype(BF)
+        analysed = (analysed * w_ref[lax.rem(me, groups)]).astype(BF)
         send2[:, pair] = analysed.reshape(harm, per, pair_width)
         for step in range(1, harm):
             backward(pair, step).start()
@@ -209,7 +210,7 @@
         ).astype(BF)
         return 0
 
-    lax.fori_loop(0, modes, spectrum, 0)
+    lax.fori_loop(0, modes, spectrum, 0, unroll=4)
 
     for step in range(1, harm):
         energy_copy(step).wait_recv()
@@ -256,16 +257,14 @@
     energy = jnp.stack([
         jnp.sum(field.astype(F32) ** 2 * energy_weight[None, None], axis=(0, 2, 3))
         for field in (velocity, magnetic)
-    ]).reshape(2 * shells, degrees)
+    ])
 
     fields = jnp.concatenate([velocity, magnetic, vorticity, current], axis=0)
     q_rows = 12 // PASSES * shells * 2
     cm = fields.reshape(PASSES, q_rows, modes, degrees).transpose(0, 2, 1, 3)
-    x = jnp.broadcast_to(jnp.asarray(cosine)[None, :], (modes, thetas))
-    sect = lax.dynamic_slice_in_dim(jnp.asarray(sectoral), me * modes, modes)
-    unsc = lax.dynamic_slice_in_dim(jnp.asarray(unscale), me * modes, modes)
-    own_weights = lax.dynamic_slice_in_dim(jnp.asarray(weights), lax.rem(me, groups) * span, span)
-    w = jnp.concatenate([own_weights, own_weights])[None, :]
+    x = jnp.asarray(np.broadcast_to(cosine[None, :], (modes, thetas)).copy())
+    cut_weights = weights.reshape(groups, 1, span)
+    w = jnp.asarray(np.concatenate([cut_weights, cut_weights], axis=2))
 
     block = min(16, modes)
     vmem = pl.BlockSpec(memory_space=pltpu.VMEM)
@@ -275,7 +274,7 @@
         name="dynamo",
         out_shape=(
             jax.ShapeDtypeStruct((modes, 12 * shells, degrees), BF),
-            jax.ShapeDtypeStruct((2 * shells, degrees), F32),
+            jax.ShapeDtypeStruct((2, shells, degrees), F32),
         ),
         in_specs=[vmem] * 8,
         out_specs=(vmem, vmem),
@@ -291,7 +290,7 @@
             pltpu.VMEM((harm, 3, 2 * modes, 2 * span), BF),
             pltpu.VMEM((modes, 12 * shells, thetas), BF),
             pltpu.VMEM((4 * shells, block, thetas), F32),
-            pltpu.VMEM((harm, 2 * shells, degrees), F32),
+            pltpu.VMEM((harm, 2, shells, degrees), F32),
             pltpu.SemaphoreType.DMA((PASSES, harm)),
             pltpu.SemaphoreType.DMA((PASSES, harm)),
             pltpu.SemaphoreType.DMA((3, harm)),
@@ -302,12 +301,12 @@
         compiler_params=pltpu.CompilerParams(
             collective_id=0, has_side_effects=True, vmem_limit_bytes=60 * 1024 * 1024
         ),
-    )(cm, x, sect, unsc, w, jnp.asarray(synthesis), jnp.asarray(analysis), energy)
+    )(cm, x, jnp.asarray(sectoral), jnp.asarray(unscale), w, jnp.asarray(synthesis), jnp.asarray(analysis), energy)
 
     spectra = spectra.transpose(1, 0, 2).reshape(6, shells, 2, modes, degrees)
     rimmed = with_halo(spectra[3:], "rad").astype(F32)
     gradient = ((rimmed[:, 2:] - rimmed[:, :-2]) * 0.5).astype(BF)
-    return spectra[:3], gradient, total.reshape(2, shells, degrees)
+    return spectra[:3], gradient, total
 
 
 def solution(mesh):

time: 130 us -> 121 us (0.931)
  Pallas kernels: 111 us -> 105 us
  local copies, waits for them, and re-layouts: 8.11 us -> 4.76 us
    pallas_call x1, Pallas kernels: 111 us -> 105 us  [local(): pl.pallas_call(functools.partial(kernel, dims), name='dynamo', out_shape=...]
    dynamic_slice x2 -> x0, local copies, waits for them, and re-layouts: 1.52 us -> none  [the longest x1 1.45 us: local(): unsc = lax.dynamic_slice_in_dim(jnp.asarray(unscale), me * modes, modes)]
where the time goes in v1:
time: 121 us
  Pallas kernels  105 us (87%)
  local copies, waits for them, and re-layouts  4.76 us (4%)
  starting transfers between devices  4.33 us (4%)
  other arithmetic  3.44 us (3%)
  waiting for transfers between devices  2.69 us (2%)
    pallas_call x1, Pallas kernels, local(): pl.pallas_call(functools.partial(kernel, dims), name='dynamo', out_shape=...  105 us
    ppermute x1, waiting for transfers between devices, with_halo(): low = lax.ppermute(block[:, -1:], axis, up)  2.68 us
  transfers between devices with their start and end apart: 2, of which 1 were waited for; matrix products, arithmetic and copies ran while one was open for 1% of the time, Pallas kernels for 0%

profile of v1, /device:TPU:26, one launch (start us, length us, event | category | flops | bytes accessed | tf_op | source)
XLA Modules:
  0.0 120.7 jit_solution(16805155593398078496)
XLA Ops:
  0.7 1.6 %pad_maximum_fusion = bf16[12,4,2,32,256]{4,3,2,1,0:T(8,128)(2,1)S(1)} fusion(bf16[3,4,2,32,256]{4,3,2,1,0:T(8,128)(2,1)} %param.13, bf16[3,4,2,32,256]{4,3,2,1,0:T(8,128)(2,1)} %param.12, bf16[3,4,2,32,256]{4,3,2,1,0:T(8,128)(2,1)} %param.11, bf16[3,4,2,32,256]{4,3,2,1,0:T(8,128)(2,1)} %param.10), kind=kLoop, calls=%fused_computation | loop fusion | flops 2359296 | bytes 3145728 | tf_op jit(solution)/shard_map/concatenate | solution.py:262
  2.2 0.0 copy-start
  2.2 0.0 copy-start.1
  2.3 2.0 %copy.25 = bf16[2,48,32,256]{3,1,2,0:T(8,128)(2,1)} copy(bf16[2,48,32,256]{3,2,1,0:T(8,128)(2,1)S(1)} %bitcast.9) | data formatting | bytes 3145728 | tf_op jit(solution)/shard_map/reshape | solution.py:264
  4.3 0.1 select_multiply_fusion.1
  4.4 0.0 copy-done
  4.4 0.0 copy-done.1
  4.4 0.2 multiply_reduce_fusion.1
  4.6 0.6 pad_maximum_fusion.2.energy_ref
  5.3 104.8 %dynamo.1 = (bf16[32,48,256]{2,1,0:T(8,128)(2,1)}, f32[2,4,256]{2,1,0:T(4,128)}) custom-call(bf16[2,32,48,256]{3,2,1,0:T(8,128)(2,1)} %bitcast.10, f32[32,384]{1,0:T(8,128)} %constant.12.clone.x_ref, f32[256,384]{1,0:T(8,128)} %constant.33.clone.sect_ref, f32[256,384]{1,0:T(8,128)} %constant.34.clone.unscale_ref, f32[2,1,384]{2,1,0:T(1,128)} %constant.32.clone.w_ref, ...), custom_call_target="tpu_custom_call" | custom-call | tf_op jit(solution)/shard_map/dynamo/pallas_call | solution.py:272
  110.0 1.2 fusion.2
  111.2 0.1 copy.23
  111.3 1.9 %collective-permute-start.1 = (bf16[3,1,2,32,256]{4,3,2,1,0:T(8,128)(2,1)S(1)}, bf16[3,1,2,32,256]{4,3,2,1,0:T(8,128)(2,1)S(1)}, u32[]{:S(2)}, u32[]{:S(2)}) collective-permute-start(bf16[3,1,2,32,256]{4,3,2,1,0:T(8,128)(2,1)S(1)} %get-tuple-element.18), channel_id=1, source_target_pairs={{8,0},{16,8},{24,16},{9,1},{17,9},{25,17},{10,2},{18,10},{26,18},{... | collective-permute-start | bytes 294920 | tf_op jit(solution)/shard_map/ppermute | solution.py:231
  113.2 2.4 %collective-permute-start = (bf16[3,1,2,32,256]{4,3,2,1,0:T(8,128)(2,1)S(1)}, bf16[3,1,2,32,256]{4,3,2,1,0:T(8,128)(2,1)S(1)}, u32[]{:S(2)}, u32[]{:S(2)}) collective-permute-start(bf16[3,1,2,32,256]{4,3,2,1,0:T(8,128)(2,1)S(1)} %get-tuple-element.17), channel_id=1, source_target_pairs={{0,8},{8,16},{16,24},{1,9},{9,17},{17,25},{2,10},{10,18},{18,26},{... | collective-permute-start | bytes 294920 | tf_op jit(solution)/shard_map/ppermute | solution.py:230
  115.7 0.8 copy.22
  116.5 0.0 copy-start.2
  116.5 0.0 collective-permute-done.1
  116.5 2.7 %collective-permute-done = bf16[3,1,2,32,256]{4,3,2,1,0:T(8,128)(2,1)S(1)} collective-permute-done((bf16[3,1,2,32,256]{4,3,2,1,0:T(8,128)(2,1)S(1)}, bf16[3,1,2,32,256]{4,3,2,1,0:T(8,128)(2,1)S(1)}, u32[]{:S(2)}, u32[]{:S(2)}) %collective-permute-start) | collective-permute-done | bytes 98336 | tf_op jit(solution)/shard_map/ppermute | solution.py:230
  119.2 0.1 maximum_convert_fusion
  119.3 0.9 fusion.1
  120.1 0.0 copy-done.2
  120.1 0.6 copy.27
  (5 shorter events, 0.0 us)
Async XLA Ops:
  2.2 2.2 %copy-start = (bf16[3,4,2,32,256]{4,3,2,1,0:T(8,128)(2,1)S(1)}, bf16[3,4,2,32,256]{4,3,2,1,0:T(8,128)(2,1)}, u32[]{:S(2)}) copy-start(bf16[3,4,2,32,256]{4,3,2,1,0:T(8,128)(2,1)} %param.11) | copy-start | bytes 1179652
  2.2 2.2 %copy-start.1 = (bf16[3,4,2,32,256]{4,3,2,1,0:T(8,128)(2,1)S(1)}, bf16[3,4,2,32,256]{4,3,2,1,0:T(8,128)(2,1)}, u32[]{:S(2)}) copy-start(bf16[3,4,2,32,256]{4,3,2,1,0:T(8,128)(2,1)} %param.10) | copy-start | bytes 1179652
  111.3 5.2 %collective-permute-start.1 = (bf16[3,1,2,32,256]{4,3,2,1,0:T(8,128)(2,1)S(1)}, bf16[3,1,2,32,256]{4,3,2,1,0:T(8,128)(2,1)S(1)}, u32[]{:S(2)}, u32[]{:S(2)}) collective-permute-start(bf16[3,1,2,32,256]{4,3,2,1,0:T(8,128)(2,1)S(1)} %get-tuple-element.18), channel_id=1, source_target_pairs={{8,0},{16,8},{24,16},{9,1},{17,9},{25,17},{10,2},{18,10},{26,18},{... | collective-permute-start | bytes 294920 | tf_op jit(solution)/shard_map/ppermute | solution.py:231
  113.2 5.9 %collective-permute-start = (bf16[3,1,2,32,256]{4,3,2,1,0:T(8,128)(2,1)S(1)}, bf16[3,1,2,32,256]{4,3,2,1,0:T(8,128)(2,1)S(1)}, u32[]{:S(2)}, u32[]{:S(2)}) collective-permute-start(bf16[3,1,2,32,256]{4,3,2,1,0:T(8,128)(2,1)S(1)} %get-tuple-element.17), channel_id=1, source_target_pairs={{0,8},{8,16},{16,24},{1,9},{9,17},{17,25},{2,10},{10,18},{18,26},{... | collective-permute-start | bytes 294920 | tf_op jit(solution)/shard_map/ppermute | solution.py:230
  116.5 3.7 %copy-start.2 = (f32[2,4,256]{2,1,0:T(4,128)S(1)}, f32[2,4,256]{2,1,0:T(4,128)}, u32[]{:S(2)}) copy-start(f32[2,4,256]{2,1,0:T(4,128)} %get-tuple-element.28) | copy-start | bytes 24580
